TPU v7x, 256 devices: a whole 4x4x8 slice. The times are simulated.
256 devices in a mesh: region: 16 (over x, y_lo, core), patch: 16 (over z, y_hi).
Axes of the slice: x: 4, y: 4 (y_hi: 2, y_lo: 2; y = y_hi * 2 + y_lo), z: 8, core: 2. Of those that a mesh axis runs over, the one named last changes fastest.
Arguments:
- nodes: bfloat16 [65536, 512], P(('region', 'patch')), may hold values from -6 to 6
- edges: bfloat16 [524288, 512], P(('region', 'patch')), may hold values from -6 to 6
- senders: int32 [524288], P(('region', 'patch')), may hold values from 0 to 799, as said below
- receivers: int32 [524288], P(('region', 'patch')), may hold values from 0 to 767, as said below
- valid_counts: int32 [256], P(('region', 'patch')), may hold values from 512 to 2048, as said below
- hub_owner: int32 [2, 16], P(None, 'region'), may hold values from 0 to 15
- edge_in: bfloat16 [2, 3, 512, 512], replicated, may hold values from -0.15625 to 0.15625
- edge_bias: float32 [2, 512], replicated, may hold values from -3 to 3
- edge_out: bfloat16 [2, 512, 512], replicated, may hold values from -0.25 to 0.25
- edge_gain: float32 [2, 512], replicated, may hold values from 0.25 to 1.75
- edge_shift: float32 [2, 512], replicated, may hold values from -2 to 2
- node_in: bfloat16 [2, 2, 512, 512], replicated, may hold values from -0.1875 to 0.1875
- node_bias: float32 [2, 512], replicated, may hold values from -3 to 3
- node_out: bfloat16 [2, 512, 512], replicated, may hold values from -0.25 to 0.25
- node_gain: float32 [2, 512], replicated, may hold values from 0.25 to 1.75
- node_shift: float32 [2, 512], replicated, may hold values from -2 to 2
Outputs:
- nodes_out: bfloat16 [65536, 512], P(('region', 'patch'))
- edges_out: bfloat16 [524288, 512], P(('region', 'patch'))
Inputs may be any that keep to these rules, and one draw needn't show every extreme that they name: `senders`: codes below 256 name a row of the previous patch, below 512 of the own patch, below 768 of the next patch, the rest a hub row. `receivers`: codes below 256 name a row of the previous patch, below 512 of the own patch, the rest of the next patch. `valid_counts`: live slots are the first ones of a patch; some patch has all 2048 slots live.
All inputs are finite; a program needn't handle non-finite values.
Results may differ from a plain program's by a relative error of at most 0.012.
Values may be sent and summed in bfloat16 or wider, within the bound.
A program may use at most 64 MiB of HBM per device.

v0:
```python
import jax
import jax.numpy as jnp
from jax import lax
from jax.sharding import Mesh
from jax.sharding import PartitionSpec as P

HUB = 32
LAYERS = 2
PATCH = ("patch_0", "patch_1")
REGION_PATCH = ("region", "patch_0", "patch_1")
epsilon = 1e-05


def extended(cells, sides, width):
    for axis, dim in sides:
        count = lax.axis_size(axis)
        head = lax.slice_in_dim(cells, 0, width, axis=dim)
        tail = lax.slice_in_dim(cells, cells.shape[dim] - width, cells.shape[dim], axis=dim)
        cells = jnp.concatenate(
            [
                lax.ppermute(tail, axis, [(i, (i + 1) % count) for i in range(count)]),
                cells,
                lax.ppermute(head, axis, [((i + 1) % count, i) for i in range(count)]),
            ],
            axis=dim,
        )
    return cells


def broadcast_by_axis(array, axes, root):
    array = jnp.where(lax.axis_index(axes) == root, array, jnp.zeros_like(array))
    for axis in axes:
        array = lax.psum(array, axis)
    return array


def from_behind(block, axis, distance):
    devices = range(lax.axis_size(axis))
    route = [((i - distance) % len(devices), i) for i in devices]
    return lax.ppermute(block, axis, route)


def activate(value):
    return value / (1.0 + jnp.exp(-value))


def layer_norm(value, gain, shift):
    center = value - jnp.mean(value, axis=-1, keepdims=True)
    spread = jnp.mean(center * center, axis=-1, keepdims=True)
    return center * lax.rsqrt(spread + epsilon) * gain + shift


def update_edges(
    edge_block,
    send_codes,
    recv_codes,
    send_table,
    recv_table,
    first_weight,
    first_bias,
    second_weight,
    gain,
    shift,
):
    pre_edge = jnp.dot(edge_block, first_weight, preferred_element_type=jnp.float32)
    pre_edge = pre_edge + jnp.take(send_table, send_codes, axis=0).astype(jnp.float32)
    pre_edge = pre_edge + jnp.take(recv_table, recv_codes, axis=0).astype(jnp.float32)
    pre_edge = pre_edge + first_bias
    activated = activate(pre_edge).astype(jnp.bfloat16)
    mixed = jnp.dot(activated, second_weight, preferred_element_type=jnp.float32)
    return edge_block.astype(jnp.float32) + layer_norm(mixed, gain, shift)


def local(
    nodes,
    edges,
    senders,
    receivers,
    valid_counts,
    hub_owner,
    edge_in,
    edge_bias,
    edge_out,
    edge_gain,
    edge_shift,
    node_in,
    node_bias,
    node_out,
    node_gain,
    node_shift,
):
    node_rows = nodes.shape[0]
    features = nodes.shape[1]
    edge_rows = edges.shape[0]
    valid_rows = valid_counts[0]
    positions = lax.broadcasted_iota(jnp.int32, (edge_rows,), 0)
    is_valid = positions < valid_rows
    for layer_index in range(LAYERS):
        holder = hub_owner[layer_index, 0]
        both_weights = jnp.concatenate([edge_in[layer_index, 1], edge_in[layer_index, 2]], axis=1)
        own_proj = jnp.dot(nodes, both_weights, preferred_element_type=jnp.float32).astype(
            jnp.bfloat16
        )
        proj_table = extended(own_proj, ((PATCH, 0),), node_rows)
        hub_send = broadcast_by_axis(own_proj[:HUB, :features], PATCH, holder)
        send_table = jnp.concatenate([proj_table[:, :features], hub_send], axis=0)
        recv_table = proj_table[:, features:]
        first_weight = edge_in[layer_index, 0]
        first_bias = edge_bias[layer_index]
        second_weight = edge_out[layer_index]
        gain = edge_gain[layer_index]
        shift = edge_shift[layer_index]
        updated = update_edges(
            edges,
            senders,
            receivers,
            send_table,
            recv_table,
            first_weight,
            first_bias,
            second_weight,
            gain,
            shift,
        )
        new_edges = jnp.where(is_valid[:, None], updated, 0.0).astype(jnp.bfloat16)
        edges = new_edges
        partial_value = jax.ops.segment_sum(
            edges.astype(jnp.float32), receivers, num_segments=3 * node_rows
        )
        from_next = from_behind(partial_value[:node_rows].astype(jnp.bfloat16), PATCH, -1).astype(
            jnp.float32
        )
        from_prev = from_behind(
            partial_value[2 * node_rows :].astype(jnp.bfloat16), PATCH, 1
        ).astype(jnp.float32)
        aggregate = (from_prev + partial_value[node_rows : 2 * node_rows] + from_next).astype(
            jnp.bfloat16
        )
        pre_node = jnp.dot(nodes, node_in[layer_index, 0], preferred_element_type=jnp.float32)
        pre_node = pre_node + jnp.dot(
            aggregate, node_in[layer_index, 1], preferred_element_type=jnp.float32
        )
        pre_node = pre_node + node_bias[layer_index]
        node_act = activate(pre_node).astype(jnp.bfloat16)
        node_mixed = jnp.dot(node_act, node_out[layer_index], preferred_element_type=jnp.float32)
        nodes = (
            nodes.astype(jnp.float32)
            + layer_norm(node_mixed, node_gain[layer_index], node_shift[layer_index])
        ).astype(jnp.bfloat16)
    return (nodes, edges)


def solution(mesh):
    torus = Mesh(mesh.devices.reshape(mesh.shape["region"], 8, 2), ("region", "patch_0", "patch_1"))
    return jax.shard_map(
        local,
        mesh=torus,
        in_specs=(
            P(REGION_PATCH, None),
            P(REGION_PATCH, None),
            P(REGION_PATCH),
            P(REGION_PATCH),
            P(REGION_PATCH),
            P(None, "region"),
            P(),
            P(),
            P(),
            P(),
            P(),
            P(),
            P(),
            P(),
            P(),
            P(),
        ),
        out_specs=(P(REGION_PATCH, None), P(REGION_PATCH, None)),
        check_vma=False,
    )
```

profile of v0, /device:TPU:4, one launch (start us, length us, event | category | flops | bytes accessed | tf_op | source)
XLA Modules:
  0.0 243.9 jit_solution(373921147333139942)
XLA Ops:
  0.6 2.7 %slice_bitcast_fusion.1 = (bf16[512,512]{1,0:T(8,128)(2,1)}, bf16[512,512]{1,0:T(8,128)(2,1)S(1)}, bf16[512,512]{1,0:T(8,128)(2,1)S(1)}, bf16[512,512]{1,0:T(8,128)(2,1)}) fusion(bf16[2,3,512,512]{3,2,1,0:T(8,128)(2,1)} %param.26), kind=kLoop, calls=%fused_computation.66 | loop fusion | bytes 4194304 | tf_op jit(solution)/shard_map/squeeze | solution.py:100
  3.4 0.0 copy-start.11
  3.4 0.0 copy-start.12
  3.4 0.0 copy-start.5
  3.4 0.4 fusion.6
  3.9 3.3 %collective-permute-start = (bf16[256,1024]{1,0:T(8,128)(2,1)S(1)}, bf16[256,1024]{1,0:T(8,128)(2,1)S(1)}, u32[]{:S(2)}, u32[]{:S(2)}) collective-permute-start(bf16[256,1024]{1,0:T(8,128)(2,1)S(1)} %fusion.6), channel_id=1, source_target_pairs={{0,1},{1,2},{2,3},{3,4},{4,5},{5,6},{6,7},{7,8},{8,9},{9,10},{10,1... | collective-permute-start | bytes 1572872 | tf_op jit(solution)/shard_map/ppermute | solution.py:21
  7.1 5.4 %collective-permute-start.1 = (bf16[256,1024]{1,0:T(8,128)(2,1)S(1)}, bf16[256,1024]{1,0:T(8,128)(2,1)}, u32[]{:S(2)}, u32[]{:S(2)}) collective-permute-start(bf16[256,1024]{1,0:T(8,128)(2,1)S(1)} %fusion.6), channel_id=1, source_target_pairs={{1,0},{2,1},{3,2},{4,3},{5,4},{6,5},{7,6},{8,7},{9,8},{10,9},{11,1... | collective-permute-start | bytes 1572872 | tf_op jit(solution)/shard_map/ppermute | solution.py:23
  12.5 0.6 fusion.91
  13.8 34.5 %psum.28 = bf16[32,512]{1,0:T(8,128)(2,1)S(1)} all-reduce(bf16[32,512]{1,0:T(8,128)(2,1)S(1)} %slice_select_fusion.1), channel_id=1, replica_groups=mesh['region'=16,'patch_0'=8,'patch_1'=2] {'patch_0'}, use_global_device_ids=true, to_apply=%region_0.1 | all-reduce | flops 16384 | bytes 65536 | tf_op jit(solution)/shard_map/psum | solution.py:33
  48.4 8.4 %psum.29 = bf16[32,512]{1,0:T(8,128)(2,1)S(1)} all-reduce(bf16[32,512]{1,0:T(8,128)(2,1)S(1)} %psum.28), channel_id=1, replica_groups=mesh['region'=16,'patch_0'=8,'patch_1'=2] {'patch_1'}, use_global_device_ids=true, to_apply=%region_1.2 | all-reduce | flops 16384 | bytes 65536 | tf_op jit(solution)/shard_map/psum | solution.py:33
  57.5 0.0 copy-start.13
  57.6 0.0 copy-start.14
  57.6 0.0 copy-start.9
  57.6 2.4 copy.20
  60.1 0.0 collective-permute-done
  60.1 1.2 pad_maximum_fusion
  61.2 0.1 fusion.82
  61.3 0.1 pad_maximum_fusion.2
  61.4 9.2 %gather_fusion = bf16[2048,512]{1,0:T(8,128)(2,1)} fusion(bf16[800,512]{1,0:T(8,128)(2,1)S(1)} %pad_maximum_fusion.2, s32[2048]{0:T(1024)S(1)} %fusion.71), kind=kCustom, calls=%fused_computation.clone | custom fusion | bytes 4202496 | tf_op jit(solution)/shard_map/jit(_take)/gather | solution.py:66
  70.6 9.2 %gather_fusion.1 = bf16[2048,512]{1,0:T(8,128)(2,1)} fusion(bf16[768,512]{1,0:T(8,128)(2,1)S(1)} %get-tuple-element.15, s32[2048]{0:T(1024)S(1)} %fusion.72), kind=kCustom, calls=%fused_computation.1.clone | custom fusion | bytes 4202496 | tf_op jit(solution)/shard_map/jit(_take)/gather | solution.py:67
  79.8 6.6 %fusion.92 = (f32[2048]{0:T(1024)S(1)}, f32[2048,512]{0,1:T(8,128)}) fusion(bf16[2,512,512]{2,1,0:T(8,128)(2,1)} %param.28, bf16[2048,512]{1,0:T(8,128)(2,1)} %gather_fusion.1, bf16[2048,512]{1,0:T(8,128)(2,1)S(1)} %copy-done.4, f32[512]{0:T(512)S(1)} %bitcast.99, pred[2048]{0:T(1024)(128)(4,1)S(1)} %get-tuple-element.42, ...), kind=kOutput, calls=%fused_computation.119 | convolution fusion | flops 2160064512 | bytes 11548672 | tf_op jit(solution)/shard_map/dot_general | solution.py:70
  86.4 2.8 %multiply_reduce_fusion.1 = f32[2048]{0:T(1024)S(1)} fusion(f32[2048,512]{0,1:T(8,128)} %get-tuple-element.35, f32[2048]{0:T(1024)S(1)} %broadcast_multiply_fusion.1), kind=kLoop, calls=%fused_computation.10 | loop fusion | flops 3143680 | bytes 4210688 | tf_op jit(solution)/shard_map/reduce_sum | solution.py:49
  89.2 0.6 copy-done.3
  89.9 2.8 %select_convert_fusion.1 = bf16[2048,512]{0,1:T(8,128)(2,1)S(1)} fusion(bf16[2048,512]{0,1:T(8,128)(2,1)} %copy.20, f32[2048,512]{0,1:T(8,128)S(1)} %copy-done.3, f32[512]{0:T(512)S(1)} %bitcast.93, f32[512]{0:T(512)S(1)} %bitcast.94, f32[2048]{0:T(1024)S(1)} %add_rsqrt_fusion.1, f32[2048]{0:T(1024)S(1)} %broadcast_multiply_fusion.1, ...), kind=kLoop, calls=%fused_computation.9 | loop fusion | flops 8388608 | bytes 8411136 | tf_op jit(solution)/shard_map/convert_element_type | solution.py:125
  92.6 3.1 %copy.21 = f32[2048,512]{1,0:T(8,128)} copy(bf16[2048,512]{0,1:T(8,128)(2,1)S(1)} %select_convert_fusion.1) | data formatting | bytes 6291456 | tf_op jit(solution)/shard_map/convert_element_type | solution.py:128
  95.7 14.4 %scatter_custom_fusion = f32[768,512]{1,0:T(8,128)} fusion(s32[2048]{0:T(1024)S(1)} %copy-done.9, f32[2048,512]{1,0:T(8,128)} %copy.21, f32[]{:T(128)} %constant.25.clone.1), kind=kCustom, calls=%fused_computation.37 | custom fusion | flops 1048576 | bytes 1573376 | tf_op jit(solution)/shard_map/scatter-add | solution.py:127
  110.1 1.7 convert.8
  111.8 3.5 %collective-permute-start.2 = (bf16[256,512]{1,0:T(8,128)(2,1)S(1)}, bf16[256,512]{1,0:T(8,128)(2,1)S(1)}, u32[]{:S(2)}, u32[]{:S(2)}) collective-permute-start(bf16[256,512]{1,0:T(8,128)(2,1)S(1)} %get-tuple-element.18), channel_id=1, source_target_pairs={{15,0},{0,1},{1,2},{2,3},{3,4},{4,5},{5,6},{6,7},{7,8},{8,9},{9,10... | collective-permute-start | bytes 786440 | tf_op jit(solution)/shard_map/ppermute | solution.py:40
  115.4 2.2 collective-permute-start.3
  117.6 0.3 fusion.39
  117.9 4.2 %collective-permute-done.2 = bf16[256,512]{1,0:T(8,128)(2,1)S(1)} collective-permute-done((bf16[256,512]{1,0:T(8,128)(2,1)S(1)}, bf16[256,512]{1,0:T(8,128)(2,1)S(1)}, u32[]{:S(2)}, u32[]{:S(2)}) %collective-permute-start.2) | collective-permute-done | bytes 262176 | tf_op jit(solution)/shard_map/ppermute | solution.py:40
  122.1 2.6 %collective-permute-done.3 = bf16[256,512]{1,0:T(8,128)(2,1)S(1)} collective-permute-done((bf16[256,512]{1,0:T(8,128)(2,1)S(1)}, bf16[256,512]{1,0:T(8,128)(2,1)S(1)}, u32[]{:S(2)}, u32[]{:S(2)}) %collective-permute-start.3) | collective-permute-done | bytes 262176 | tf_op jit(solution)/shard_map/ppermute | solution.py:40
  124.7 0.7 copy-done.18
  125.4 2.0 fusion.95
  127.5 0.2 multiply_reduce_fusion.3
  127.7 0.2 add_convert_fusion.1
  127.9 1.6 convolution_convert_fusion.1
  129.5 1.5 collective-permute-start.4
  131.0 4.2 %collective-permute-start.5 = (bf16[256,1024]{1,0:T(8,128)(2,1)S(1)}, bf16[256,1024]{1,0:T(8,128)(2,1)S(1)}, u32[]{:S(2)}, u32[]{:S(2)}) collective-permute-start(bf16[256,1024]{1,0:T(8,128)(2,1)S(1)} %convolution_convert_fusion.1), channel_id=1, source_target_pairs={{1,0},{2,1},{3,2},{4,3},{5,4},{6,5},{7,6},{8,7},{9,8},{10,9},{11,1... | collective-permute-start | bytes 1572872 | tf_op jit(solution)/shard_map/ppermute | solution.py:23
  135.9 30.6 %psum.30 = bf16[32,512]{1,0:T(8,128)(2,1)S(1)} all-reduce(bf16[32,512]{1,0:T(8,128)(2,1)S(1)} %slice_select_fusion), channel_id=1, replica_groups=mesh['region'=16,'patch_0'=8,'patch_1'=2] {'patch_0'}, use_global_device_ids=true, to_apply=%region_7.10 | all-reduce | flops 16384 | bytes 65536 | tf_op jit(solution)/shard_map/psum | solution.py:33
  166.5 8.4 %psum.31 = bf16[32,512]{1,0:T(8,128)(2,1)S(1)} all-reduce(bf16[32,512]{1,0:T(8,128)(2,1)S(1)} %psum.30), channel_id=1, replica_groups=mesh['region'=16,'patch_0'=8,'patch_1'=2] {'patch_1'}, use_global_device_ids=true, to_apply=%region_8.11 | all-reduce | flops 16384 | bytes 65536 | tf_op jit(solution)/shard_map/psum | solution.py:33
  174.9 0.0 collective-permute-done.4
  175.0 0.1 pad_maximum_fusion.1
  175.1 0.1 fusion.81
  175.2 0.1 pad_maximum_fusion.3
  175.3 9.2 %gather_fusion.2 = bf16[2048,512]{1,0:T(8,128)(2,1)} fusion(bf16[800,512]{1,0:T(8,128)(2,1)S(1)} %pad_maximum_fusion.3, s32[2048]{0:T(1024)S(1)} %fusion.71), kind=kCustom, calls=%fused_computation.2.clone | custom fusion | bytes 4202496 | tf_op jit(solution)/shard_map/jit(_take)/gather | solution.py:66
  184.5 9.2 %gather_fusion.3 = bf16[2048,512]{1,0:T(8,128)(2,1)} fusion(bf16[768,512]{1,0:T(8,128)(2,1)S(1)} %get-tuple-element.13, s32[2048]{0:T(1024)S(1)} %fusion.72), kind=kCustom, calls=%fused_computation.3.clone | custom fusion | bytes 4202496 | tf_op jit(solution)/shard_map/jit(_take)/gather | solution.py:67
  193.7 7.9 %fusion.100 = (f32[2048]{0:T(1024)S(1)}, f32[2048,512]{0,1:T(8,128)}) fusion(bf16[2,512,512]{2,1,0:T(8,128)(2,1)} %param.28, bf16[2048,512]{1,0:T(8,128)(2,1)} %gather_fusion.3, bf16[2048,512]{1,0:T(8,128)(2,1)} %gather_fusion.2, f32[512]{0:T(512)S(1)} %bitcast.97, pred[2048]{0:T(1024)(128)(4,1)S(1)} %get-tuple-element.42, ...), kind=kOutput, calls=%fused_computation.121 | convolution fusion | flops 2160064512 | bytes 11548672 | tf_op jit(solution)/shard_map/dot_general | solution.py:70
  201.6 2.8 %multiply_reduce_fusion = f32[2048]{0:T(1024)S(1)} fusion(f32[2048,512]{0,1:T(8,128)} %get-tuple-element.39, f32[2048]{0:T(1024)S(1)} %broadcast_multiply_fusion), kind=kLoop, calls=%fused_computation.7 | loop fusion | flops 3143680 | bytes 4210688 | tf_op jit(solution)/shard_map/reduce_sum | solution.py:49
  204.4 0.1 copy-done.2
  204.5 3.3 %select_convert_fusion = bf16[2048,512]{0,1:T(8,128)(2,1)S(1)} fusion(f32[2048,512]{0,1:T(8,128)} %get-tuple-element.39, f32[512]{0:T(512)S(1)} %bitcast.89, f32[512]{0:T(512)S(1)} %bitcast.90, f32[2048]{0:T(1024)S(1)} %add_rsqrt_fusion, f32[2048]{0:T(1024)S(1)} %broadcast_multiply_fusion, pred[2048]{0:T(1024)(128)(4,1)S(1)} %iota_compare_fusion, ...), kind=kLoop, calls=%fused_computation.6 | loop fusion | flops 8388608 | bytes 8411136 | tf_op jit(solution)/shard_map/convert_element_type | solution.py:125
  207.8 3.0 %copy.22 = f32[2048,512]{1,0:T(8,128)} copy(bf16[2048,512]{0,1:T(8,128)(2,1)S(1)} %select_convert_fusion) | data formatting | bytes 6291456 | tf_op jit(solution)/shard_map/convert_element_type | solution.py:128
  210.8 14.5 %scatter_custom_fusion.1 = f32[768,512]{1,0:T(8,128)} fusion(s32[2048]{0:T(1024)S(1)} %copy-done.9, f32[2048,512]{1,0:T(8,128)} %copy.22, f32[]{:T(128)} %constant.25.clone.1), kind=kCustom, calls=%fused_computation.35 | custom fusion | flops 1048576 | bytes 1573376 | tf_op jit(solution)/shard_map/scatter-add | solution.py:127
  225.3 1.5 convert.9
  226.8 0.7 fusion.83
  227.5 3.5 %collective-permute-start.6 = (bf16[256,512]{1,0:T(8,128)(2,1)}, bf16[256,512]{1,0:T(8,128)(2,1)S(1)}, u32[]{:S(2)}, u32[]{:S(2)}) collective-permute-start(bf16[256,512]{1,0:T(8,128)(2,1)} %get-tuple-element.16), channel_id=1, source_target_pairs={{15,0},{0,1},{1,2},{2,3},{3,4},{4,5},{5,6},{6,7},{7,8},{8,9},{9,10... | collective-permute-start | bytes 786440 | tf_op jit(solution)/shard_map/ppermute | solution.py:40
  231.0 2.2 collective-permute-start.7
  233.2 1.3 fusion.31
  234.5 2.5 %copy.23 = bf16[2048,512]{1,0:T(8,128)(2,1)} copy(bf16[2048,512]{0,1:T(8,128)(2,1)S(1)} %select_convert_fusion) | data formatting | bytes 4194304
  237.0 1.0 collective-permute-done.6
  238.0 2.6 %collective-permute-done.7 = bf16[256,512]{1,0:T(8,128)(2,1)} collective-permute-done((bf16[256,512]{1,0:T(8,128)(2,1)S(1)}, bf16[256,512]{1,0:T(8,128)(2,1)}, u32[]{:S(2)}, u32[]{:S(2)}) %collective-permute-start.7) | collective-permute-done | bytes 262176 | tf_op jit(solution)/shard_map/ppermute | solution.py:40
  240.6 2.1 fusion.103
  242.8 0.2 multiply_reduce_fusion.2
  243.0 0.9 add_convert_fusion
  (52 shorter events, 0.2 us)
Async XLA Ops:
  0.6 2.8 %copy-start.6 = (bf16[256,512]{1,0:T(8,128)(2,1)S(1)}, bf16[256,512]{1,0:T(8,128)(2,1)}, u32[]{:S(2)}) copy-start(bf16[256,512]{1,0:T(8,128)(2,1)} %param.20) | copy-start | bytes 786436
  3.4 9.2 %copy-start.16 = (s32[2,1]{0,1:T(1,128)S(1)}, s32[2,1]{0,1:T(1,128)}, u32[]{:S(2)}) copy-start(s32[2,1]{0,1:T(1,128)} %param.25) | copy-start | bytes 28
  3.4 53.4 %copy-start.8 = (s32[2048]{0:T(1024)S(1)}, s32[2048]{0:T(1024)}, u32[]{:S(2)}) copy-start(s32[2048]{0:T(1024)} %param.22) | copy-start | bytes 24580
  3.4 53.4 %copy-start.10 = (f32[2,512]{1,0:T(2,128)S(1)}, f32[2,512]{1,0:T(2,128)}, u32[]{:S(2)}) copy-start(f32[2,512]{1,0:T(2,128)} %param.27) | copy-start | bytes 12292
  3.4 53.5 %copy-start.11 = (f32[2,512]{1,0:T(2,128)S(1)}, f32[2,512]{1,0:T(2,128)}, u32[]{:S(2)}) copy-start(f32[2,512]{1,0:T(2,128)} %param.30) | copy-start | bytes 12292
  3.4 53.5 %copy-start.12 = (f32[2,512]{1,0:T(2,128)S(1)}, f32[2,512]{1,0:T(2,128)}, u32[]{:S(2)}) copy-start(f32[2,512]{1,0:T(2,128)} %param.29) | copy-start | bytes 12292
  3.4 54.1 %copy-start.5 = (bf16[2048,512]{1,0:T(8,128)(2,1)S(1)}, bf16[2048,512]{1,0:T(8,128)(2,1)}, u32[]{:S(2)}) copy-start(bf16[2048,512]{1,0:T(8,128)(2,1)} %param.21) | copy-start | bytes 6291460
  3.9 56.2 %collective-permute-start = (bf16[256,1024]{1,0:T(8,128)(2,1)S(1)}, bf16[256,1024]{1,0:T(8,128)(2,1)S(1)}, u32[]{:S(2)}, u32[]{:S(2)}) collective-permute-start(bf16[256,1024]{1,0:T(8,128)(2,1)S(1)} %fusion.6), channel_id=1, source_target_pairs={{0,1},{1,2},{2,3},{3,4},{4,5},{5,6},{6,7},{7,8},{8,9},{9,10},{10,1... | collective-permute-start | bytes 1572872 | tf_op jit(solution)/shard_map/ppermute | solution.py:21
  7.1 52.9 %collective-permute-start.1 = (bf16[256,1024]{1,0:T(8,128)(2,1)S(1)}, bf16[256,1024]{1,0:T(8,128)(2,1)}, u32[]{:S(2)}, u32[]{:S(2)}) collective-permute-start(bf16[256,1024]{1,0:T(8,128)(2,1)S(1)} %fusion.6), channel_id=1, source_target_pairs={{1,0},{2,1},{3,2},{4,3},{5,4},{6,5},{7,6},{8,7},{9,8},{10,9},{11,1... | collective-permute-start | bytes 1572872 | tf_op jit(solution)/shard_map/ppermute | solution.py:23
  57.5 2.4 copy-start.13
  57.6 2.4 copy-start.14
  57.6 2.4 %copy-start.9 = (s32[2048]{0:T(1024)S(1)}, s32[2048]{0:T(1024)}, u32[]{:S(2)}) copy-start(s32[2048]{0:T(1024)} %param.23) | copy-start | bytes 24580
  70.6 9.2 %copy-start.4 = (bf16[2048,512]{1,0:T(8,128)(2,1)S(1)}, bf16[2048,512]{1,0:T(8,128)(2,1)}, u32[]{:S(2)}) copy-start(bf16[2048,512]{1,0:T(8,128)(2,1)} %gather_fusion) | copy-start | bytes 6291460
  86.4 3.4 %copy-start.3 = (f32[2048,512]{0,1:T(8,128)S(1)}, f32[2048,512]{0,1:T(8,128)}, u32[]{:S(2)}) copy-start(f32[2048,512]{0,1:T(8,128)} %get-tuple-element.35) | copy-start | bytes 12582916
  92.6 3.1 %copy-start = (bf16[2048,512]{0,1:T(8,128)(2,1)}, bf16[2048,512]{0,1:T(8,128)(2,1)S(1)}, u32[]{:S(2)}) copy-start(bf16[2048,512]{0,1:T(8,128)(2,1)S(1)} %select_convert_fusion.1) | copy-start | bytes 6291460
  110.1 7.4 %copy-start.15 = (f32[2,512]{1,0:T(2,128)S(1)}, f32[2,512]{1,0:T(2,128)}, u32[]{:S(2)}) copy-start(f32[2,512]{1,0:T(2,128)} %param.35) | copy-start | bytes 12292
  110.1 7.4 %copy-start.7 = (bf16[2,2,512,512]{3,2,1,0:T(8,128)(2,1)S(1)}, bf16[2,2,512,512]{3,2,1,0:T(8,128)(2,1)}, u32[]{:S(2)}) copy-start(bf16[2,2,512,512]{3,2,1,0:T(8,128)(2,1)} %param.31) | copy-start | bytes 6291460
  111.8 10.2 %collective-permute-start.2 = (bf16[256,512]{1,0:T(8,128)(2,1)S(1)}, bf16[256,512]{1,0:T(8,128)(2,1)S(1)}, u32[]{:S(2)}, u32[]{:S(2)}) collective-permute-start(bf16[256,512]{1,0:T(8,128)(2,1)S(1)} %get-tuple-element.18), channel_id=1, source_target_pairs={{15,0},{0,1},{1,2},{2,3},{3,4},{4,5},{5,6},{6,7},{7,8},{8,9},{9,10... | collective-permute-start | bytes 786440 | tf_op jit(solution)/shard_map/ppermute | solution.py:40
  115.4 9.3 %collective-permute-start.3 = (bf16[256,512]{1,0:T(8,128)(2,1)S(1)}, bf16[256,512]{1,0:T(8,128)(2,1)S(1)}, u32[]{:S(2)}, u32[]{:S(2)}) collective-permute-start(bf16[256,512]{1,0:T(8,128)(2,1)S(1)} %get-tuple-element.19), channel_id=1, source_target_pairs={{1,0},{2,1},{3,2},{4,3},{5,4},{6,5},{7,6},{8,7},{9,8},{10,9},{11,1... | collective-permute-start | bytes 786440 | tf_op jit(solution)/shard_map/ppermute | solution.py:40
  122.1 2.6 %copy-start.17 = (bf16[256,512]{1,0:T(8,128)(2,1)}, bf16[256,512]{1,0:T(8,128)(2,1)S(1)}, u32[]{:S(2)}) copy-start(bf16[256,512]{1,0:T(8,128)(2,1)S(1)} %collective-permute-done.2) | copy-start | bytes 786436
  124.7 0.7 copy-start.18
  129.5 45.4 %collective-permute-start.4 = (bf16[256,1024]{1,0:T(8,128)(2,1)S(1)}, bf16[256,1024]{1,0:T(8,128)(2,1)S(1)}, u32[]{:S(2)}, u32[]{:S(2)}) collective-permute-start(bf16[256,1024]{1,0:T(8,128)(2,1)S(1)} %convolution_convert_fusion.1), channel_id=1, source_target_pairs={{0,1},{1,2},{2,3},{3,4},{4,5},{5,6},{6,7},{7,8},{8,9},{9,10},{10,1... | collective-permute-start | bytes 1572872 | tf_op jit(solution)/shard_map/ppermute | solution.py:21
  131.0 43.9 %collective-permute-start.5 = (bf16[256,1024]{1,0:T(8,128)(2,1)S(1)}, bf16[256,1024]{1,0:T(8,128)(2,1)S(1)}, u32[]{:S(2)}, u32[]{:S(2)}) collective-permute-start(bf16[256,1024]{1,0:T(8,128)(2,1)S(1)} %convolution_convert_fusion.1), channel_id=1, source_target_pairs={{1,0},{2,1},{3,2},{4,3},{5,4},{6,5},{7,6},{8,7},{9,8},{10,9},{11,1... | collective-permute-start | bytes 1572872 | tf_op jit(solution)/shard_map/ppermute | solution.py:23
  184.5 9.2 %copy-start.1 = (bf16[2048,512]{0,1:T(8,128)(2,1)S(1)}, bf16[2048,512]{0,1:T(8,128)(2,1)}, u32[]{:S(2)}) copy-start(bf16[2048,512]{0,1:T(8,128)(2,1)} %copy-done) | copy-start | bytes 6291460
  201.6 2.9 %copy-start.2 = (bf16[2048,512]{0,1:T(8,128)(2,1)S(1)}, bf16[2048,512]{0,1:T(8,128)(2,1)}, u32[]{:S(2)}) copy-start(bf16[2048,512]{0,1:T(8,128)(2,1)} %copy-done) | copy-start | bytes 6291460
  227.5 10.5 %collective-permute-start.6 = (bf16[256,512]{1,0:T(8,128)(2,1)}, bf16[256,512]{1,0:T(8,128)(2,1)S(1)}, u32[]{:S(2)}, u32[]{:S(2)}) collective-permute-start(bf16[256,512]{1,0:T(8,128)(2,1)} %get-tuple-element.16), channel_id=1, source_target_pairs={{15,0},{0,1},{1,2},{2,3},{3,4},{4,5},{5,6},{6,7},{7,8},{8,9},{9,10... | collective-permute-start | bytes 786440 | tf_op jit(solution)/shard_map/ppermute | solution.py:40
  231.0 9.6 %collective-permute-start.7 = (bf16[256,512]{1,0:T(8,128)(2,1)S(1)}, bf16[256,512]{1,0:T(8,128)(2,1)}, u32[]{:S(2)}, u32[]{:S(2)}) collective-permute-start(bf16[256,512]{1,0:T(8,128)(2,1)S(1)} %get-tuple-element.17), channel_id=1, source_target_pairs={{1,0},{2,1},{3,2},{4,3},{5,4},{6,5},{7,6},{8,7},{9,8},{10,9},{11,1... | collective-permute-start | bytes 786440 | tf_op jit(solution)/shard_map/ppermute | solution.py:40
where the time goes:
time: 244 us
  blocking collectives  82 us (34%)
  local copies, waits for them, and re-layouts  53.6 us (22%)
  other arithmetic  46.7 us (19%)
  starting transfers between devices  25.7 us (11%)
  matrix products  22.4 us (9%)
  waiting for transfers between devices  10.5 us (4%)
  between operations  3.04 us (1%)
    psum x4, blocking collectives, broadcast_by_axis(): array = lax.psum(array, axis)  82 us
    scatter-add x2, other arithmetic, local(): jax.ops.segment_sum(edges.astype(jnp.float32), receivers, num_segments=3...  28.9 us
    gather x2, local copies, waits for them, and re-layouts, update_edges(): jnp.take(recv_table, recv_codes, axis=0).astype(jnp.float32)  18.4 us
    gather x2, local copies, waits for them, and re-layouts, update_edges(): jnp.take(send_table, send_codes, axis=0).astype(jnp.float32)  18.4 us
    dot_general x2, matrix products, update_edges(): jnp.dot(activated, second_weight, preferred_element_type=jnp.float32)  14.5 us
    ppermute x4, starting transfers between devices, from_behind(): return lax.ppermute(block, axis, route)  11.4 us
    ppermute x4, waiting for transfers between devices, from_behind(): return lax.ppermute(block, axis, route)  10.5 us
    ppermute x2, starting transfers between devices, extended(): lax.ppermute(head, axis, [((i + 1) % count, i) for i in range(count)])  9.59 us
  transfers between devices with their start and end apart: 8, of which 4 were waited for; matrix products, arithmetic and copies ran while one was open for 3% of the time, Pallas kernels for 0%

commit v1 on v0

--- a/solution.py
+++ b/solution.py
@@ -30,7 +30,7 @@
 def broadcast_by_axis(array, axes, root):
     array = jnp.where(lax.axis_index(axes) == root, array, jnp.zeros_like(array))
     for axis in axes:
-        array = lax.psum(array, axis)
+        array = jnp.sum(lax.all_gather(array, axis), axis=0)
     return array
 
 

time: 244 us -> 230 us (0.943)
  blocking collectives: 82 us -> 68.4 us
    psum x4 -> x0, blocking collectives: 82 us -> none  [broadcast_by_axis(): array = lax.psum(array, axis)]
    all_gather x0 -> x4, blocking collectives: none -> 68.4 us  [broadcast_by_axis(): array = jnp.sum(lax.all_gather(array, axis), axis=0)]
where the time goes in v1:
time: 230 us
  blocking collectives  68.4 us (30%)
  local copies, waits for them, and re-layouts  53.5 us (23%)
  other arithmetic  47 us (20%)
  starting transfers between devices  25.7 us (11%)
  matrix products  22.4 us (10%)
  waiting for transfers between devices  9.43 us (4%)
  between operations  3.04 us (1%)
    all_gather x4, blocking collectives, broadcast_by_axis(): array = jnp.sum(lax.all_gather(array, axis), axis=0)  68.4 us
    scatter-add x2, other arithmetic, local(): jax.ops.segment_sum(edges.astype(jnp.float32), receivers, num_segments=3...  28.9 us
    gather x2, local copies, waits for them, and re-layouts, update_edges(): jnp.take(recv_table, recv_codes, axis=0).astype(jnp.float32)  18.4 us
    gather x2, local copies, waits for them, and re-layouts, update_edges(): jnp.take(send_table, send_codes, axis=0).astype(jnp.float32)  18.4 us
    dot_general x2, matrix products, update_edges(): jnp.dot(activated, second_weight, preferred_element_type=jnp.float32)  14.5 us
    ppermute x4, starting transfers between devices, from_behind(): return lax.ppermute(block, axis, route)  11.4 us
    ppermute x4, waiting for transfers between devices, from_behind(): return lax.ppermute(block, axis, route)  9.42 us
    ppermute x2, starting transfers between devices, extended(): lax.ppermute(head, axis, [((i + 1) % count, i) for i in range(count)])  9.4 us
  transfers between devices with their start and end apart: 8, of which 4 were waited for; matrix products, arithmetic and copies ran while one was open for 3% of the time, Pallas kernels for 0%

profile of v1, /device:TPU:4, one launch (start us, length us, event | category | flops | bytes accessed | tf_op | source)
XLA Modules:
  0.0 229.5 jit_solution(13480119820016155338)
XLA Ops:
  0.6 2.7 %slice_bitcast_fusion.1 = (bf16[512,512]{1,0:T(8,128)(2,1)}, bf16[512,512]{1,0:T(8,128)(2,1)S(1)}, bf16[512,512]{1,0:T(8,128)(2,1)S(1)}, bf16[512,512]{1,0:T(8,128)(2,1)}) fusion(bf16[2,3,512,512]{3,2,1,0:T(8,128)(2,1)} %param.26), kind=kLoop, calls=%fused_computation.66 | loop fusion | bytes 4194304 | tf_op jit(solution)/shard_map/squeeze | solution.py:100
  3.3 0.0 copy-start.11
  3.4 0.0 copy-start.12
  3.4 0.0 copy-start.5
  3.4 0.4 fusion.6
  3.8 3.3 %collective-permute-start = (bf16[256,1024]{1,0:T(8,128)(2,1)S(1)}, bf16[256,1024]{1,0:T(8,128)(2,1)}, u32[]{:S(2)}, u32[]{:S(2)}) collective-permute-start(bf16[256,1024]{1,0:T(8,128)(2,1)S(1)} %fusion.6), channel_id=1, source_target_pairs={{0,1},{1,2},{2,3},{3,4},{4,5},{5,6},{6,7},{7,8},{8,9},{9,10},{10,1... | collective-permute-start | bytes 1572872 | tf_op jit(solution)/shard_map/ppermute | solution.py:21
  7.1 5.4 %collective-permute-start.1 = (bf16[256,1024]{1,0:T(8,128)(2,1)S(1)}, bf16[256,1024]{1,0:T(8,128)(2,1)}, u32[]{:S(2)}, u32[]{:S(2)}) collective-permute-start(bf16[256,1024]{1,0:T(8,128)(2,1)S(1)} %fusion.6), channel_id=1, source_target_pairs={{1,0},{2,1},{3,2},{4,3},{5,4},{6,5},{7,6},{8,7},{9,8},{10,9},{11,1... | collective-permute-start | bytes 1572872 | tf_op jit(solution)/shard_map/ppermute | solution.py:23
  12.5 0.6 fusion.91
  13.8 30.2 %all-gather = bf16[256,512]{1,0:T(8,128)(2,1)S(1)} all-gather(bf16[32,512]{1,0:T(8,128)(2,1)S(1)} %slice_select_fusion.1), channel_id=2, replica_groups=mesh['region'=16,'patch_0'=8,'patch_1'=2] {'patch_0'}, dimensions={0}, use_global_device_ids=true | all-gather | bytes 294912 | tf_op jit(solution)/shard_map/all_gather | solution.py:33
  44.1 6.1 %all-gather.1 = bf16[64,512]{1,0:T(8,128)(2,1)S(1)} all-gather(bf16[32,512]{1,0:T(8,128)(2,1)S(1)} %reduce_sum.120), channel_id=3, replica_groups=mesh['region'=16,'patch_0'=8,'patch_1'=2] {'patch_1'}, dimensions={0}, use_global_device_ids=true | all-gather | bytes 98304 | tf_op jit(solution)/shard_map/all_gather | solution.py:33
  50.9 0.0 copy-start.13
  50.9 0.0 copy-start.14
  50.9 0.0 copy-start.9
  51.0 2.4 %copy.24 = bf16[2048,512]{0,1:T(8,128)(2,1)} copy(bf16[2048,512]{1,0:T(8,128)(2,1)S(1)} %copy-done.5) | data formatting | bytes 4194304 | tf_op args[1]
  53.4 0.0 collective-permute-done
  53.4 0.0 collective-permute-done.1
  53.5 1.3 pad_maximum_fusion
  54.8 0.1 fusion.82
  54.9 0.1 pad_maximum_fusion.2
  54.9 9.2 %gather_fusion = bf16[2048,512]{1,0:T(8,128)(2,1)} fusion(bf16[800,512]{1,0:T(8,128)(2,1)S(1)} %pad_maximum_fusion.2, s32[2048]{0:T(1024)S(1)} %fusion.71), kind=kCustom, calls=%fused_computation.clone | custom fusion | bytes 4202496 | tf_op jit(solution)/shard_map/jit(_take)/gather | solution.py:66
  64.1 9.2 %gather_fusion.1 = bf16[2048,512]{1,0:T(8,128)(2,1)} fusion(bf16[768,512]{1,0:T(8,128)(2,1)S(1)} %get-tuple-element.17, s32[2048]{0:T(1024)S(1)} %fusion.72), kind=kCustom, calls=%fused_computation.1.clone | custom fusion | bytes 4202496 | tf_op jit(solution)/shard_map/jit(_take)/gather | solution.py:67
  73.3 6.6 %fusion.92 = (f32[2048]{0:T(1024)S(1)}, f32[2048,512]{0,1:T(8,128)}) fusion(bf16[2,512,512]{2,1,0:T(8,128)(2,1)} %param.28, bf16[2048,512]{1,0:T(8,128)(2,1)} %gather_fusion.1, bf16[2048,512]{1,0:T(8,128)(2,1)S(1)} %copy-done.4, f32[512]{0:T(512)S(1)} %bitcast.107, pred[2048]{0:T(1024)(128)(4,1)S(1)} %get-tuple-element.44, ...), kind=kOutput, calls=%fused_computation.119 | convolution fusion | flops 2160064512 | bytes 11548672 | tf_op jit(solution)/shard_map/dot_general | solution.py:70
  79.9 2.8 %multiply_reduce_fusion.1 = f32[2048]{0:T(1024)S(1)} fusion(f32[2048,512]{0,1:T(8,128)} %get-tuple-element.37, f32[2048]{0:T(1024)S(1)} %broadcast_multiply_fusion.1), kind=kLoop, calls=%fused_computation.10 | loop fusion | flops 3143680 | bytes 4210688 | tf_op jit(solution)/shard_map/reduce_sum | solution.py:49
  82.7 0.6 copy-done.3
  83.4 2.8 %select_convert_fusion.1 = bf16[2048,512]{0,1:T(8,128)(2,1)S(1)} fusion(bf16[2048,512]{0,1:T(8,128)(2,1)} %copy.24, f32[2048,512]{0,1:T(8,128)S(1)} %copy-done.3, f32[512]{0:T(512)S(1)} %bitcast.102, f32[512]{0:T(512)S(1)} %bitcast.101, f32[2048]{0:T(1024)S(1)} %add_rsqrt_fusion.1, f32[2048]{0:T(1024)S(1)} %broadcast_multiply_fusion.1, ...), kind=kLoop, calls=%fused_computation.9 | loop fusion | flops 8388608 | bytes 8411136 | tf_op jit(solution)/shard_map/convert_element_type | solution.py:125
  86.2 3.1 %copy.25 = f32[2048,512]{1,0:T(8,128)} copy(bf16[2048,512]{0,1:T(8,128)(2,1)S(1)} %select_convert_fusion.1) | data formatting | bytes 6291456 | tf_op jit(solution)/shard_map/convert_element_type | solution.py:128
  89.2 14.4 %scatter_custom_fusion = f32[768,512]{1,0:T(8,128)} fusion(s32[2048]{0:T(1024)S(1)} %copy-done.9, f32[2048,512]{1,0:T(8,128)} %copy.25, f32[]{:T(128)} %constant.29.clone.1), kind=kCustom, calls=%fused_computation.37 | custom fusion | flops 1048576 | bytes 1573376 | tf_op jit(solution)/shard_map/scatter-add | solution.py:127
  103.7 1.7 convert.12
  105.4 0.5 collective-permute-start.2
  105.9 5.2 %collective-permute-start.3 = (bf16[256,512]{1,0:T(8,128)(2,1)S(1)}, bf16[256,512]{1,0:T(8,128)(2,1)S(1)}, u32[]{:S(2)}, u32[]{:S(2)}) collective-permute-start(bf16[256,512]{1,0:T(8,128)(2,1)S(1)} %get-tuple-element.21), channel_id=1, source_target_pairs={{1,0},{2,1},{3,2},{4,3},{5,4},{6,5},{7,6},{8,7},{9,8},{10,9},{11,1... | collective-permute-start | bytes 786440 | tf_op jit(solution)/shard_map/ppermute | solution.py:40
  111.1 0.3 fusion.39
  111.4 4.1 %collective-permute-done.2 = bf16[256,512]{1,0:T(8,128)(2,1)S(1)} collective-permute-done((bf16[256,512]{1,0:T(8,128)(2,1)S(1)}, bf16[256,512]{1,0:T(8,128)(2,1)S(1)}, u32[]{:S(2)}, u32[]{:S(2)}) %collective-permute-start.2) | collective-permute-done | bytes 262176 | tf_op jit(solution)/shard_map/ppermute | solution.py:40
  115.5 2.3 %collective-permute-done.3 = bf16[256,512]{1,0:T(8,128)(2,1)S(1)} collective-permute-done((bf16[256,512]{1,0:T(8,128)(2,1)S(1)}, bf16[256,512]{1,0:T(8,128)(2,1)S(1)}, u32[]{:S(2)}, u32[]{:S(2)}) %collective-permute-start.3) | collective-permute-done | bytes 262176 | tf_op jit(solution)/shard_map/ppermute | solution.py:40
  117.9 0.7 copy-done.18
  118.6 2.0 fusion.95
  120.6 0.2 multiply_reduce_fusion.3
  120.8 0.2 add_convert_fusion.1
  121.0 1.6 convolution_convert_fusion.1
  122.7 1.7 collective-permute-start.4
  124.4 4.0 %collective-permute-start.5 = (bf16[256,1024]{1,0:T(8,128)(2,1)S(1)}, bf16[256,1024]{1,0:T(8,128)(2,1)S(1)}, u32[]{:S(2)}, u32[]{:S(2)}) collective-permute-start(bf16[256,1024]{1,0:T(8,128)(2,1)S(1)} %convolution_convert_fusion.1), channel_id=1, source_target_pairs={{1,0},{2,1},{3,2},{4,3},{5,4},{6,5},{7,6},{8,7},{9,8},{10,9},{11,1... | collective-permute-start | bytes 1572872 | tf_op jit(solution)/shard_map/ppermute | solution.py:23
  129.1 26.0 %all-gather.2 = bf16[256,512]{1,0:T(8,128)(2,1)S(1)} all-gather(bf16[32,512]{1,0:T(8,128)(2,1)S(1)} %slice_select_fusion), channel_id=4, replica_groups=mesh['region'=16,'patch_0'=8,'patch_1'=2] {'patch_0'}, dimensions={0}, use_global_device_ids=true | all-gather | bytes 294912 | tf_op jit(solution)/shard_map/all_gather | solution.py:33
  155.1 6.1 %all-gather.3 = bf16[64,512]{1,0:T(8,128)(2,1)S(1)} all-gather(bf16[32,512]{1,0:T(8,128)(2,1)S(1)} %reduce_sum.126), channel_id=5, replica_groups=mesh['region'=16,'patch_0'=8,'patch_1'=2] {'patch_1'}, dimensions={0}, use_global_device_ids=true | all-gather | bytes 98304 | tf_op jit(solution)/shard_map/all_gather | solution.py:33
  161.3 0.1 pad_maximum_fusion.1
  161.4 0.1 fusion.81
  161.5 0.1 pad_maximum_fusion.3
  161.6 9.2 %gather_fusion.2 = bf16[2048,512]{1,0:T(8,128)(2,1)} fusion(bf16[800,512]{1,0:T(8,128)(2,1)S(1)} %pad_maximum_fusion.3, s32[2048]{0:T(1024)S(1)} %fusion.71), kind=kCustom, calls=%fused_computation.2.clone | custom fusion | bytes 4202496 | tf_op jit(solution)/shard_map/jit(_take)/gather | solution.py:66
  170.8 9.2 %gather_fusion.3 = bf16[2048,512]{1,0:T(8,128)(2,1)} fusion(bf16[768,512]{1,0:T(8,128)(2,1)S(1)} %get-tuple-element.15, s32[2048]{0:T(1024)S(1)} %fusion.72), kind=kCustom, calls=%fused_computation.3.clone | custom fusion | bytes 4202496 | tf_op jit(solution)/shard_map/jit(_take)/gather | solution.py:67
  180.0 7.9 %fusion.100 = (f32[2048]{0:T(1024)S(1)}, f32[2048,512]{0,1:T(8,128)}) fusion(bf16[2,512,512]{2,1,0:T(8,128)(2,1)} %param.28, bf16[2048,512]{1,0:T(8,128)(2,1)} %gather_fusion.3, bf16[2048,512]{1,0:T(8,128)(2,1)} %gather_fusion.2, f32[512]{0:T(512)S(1)} %bitcast.105, pred[2048]{0:T(1024)(128)(4,1)S(1)} %get-tuple-element.44, ...), kind=kOutput, calls=%fused_computation.121 | convolution fusion | flops 2160064512 | bytes 11548672 | tf_op jit(solution)/shard_map/dot_general | solution.py:70
  187.9 2.8 %multiply_reduce_fusion = f32[2048]{0:T(1024)S(1)} fusion(f32[2048,512]{0,1:T(8,128)} %get-tuple-element.41, f32[2048]{0:T(1024)S(1)} %broadcast_multiply_fusion), kind=kLoop, calls=%fused_computation.7 | loop fusion | flops 3143680 | bytes 4210688 | tf_op jit(solution)/shard_map/reduce_sum | solution.py:49
  190.7 0.1 copy-done.2
  190.8 3.3 %select_convert_fusion = bf16[2048,512]{0,1:T(8,128)(2,1)S(1)} fusion(f32[2048,512]{0,1:T(8,128)} %get-tuple-element.41, f32[512]{0:T(512)S(1)} %bitcast.98, f32[512]{0:T(512)S(1)} %bitcast.97, f32[2048]{0:T(1024)S(1)} %add_rsqrt_fusion, f32[2048]{0:T(1024)S(1)} %broadcast_multiply_fusion, pred[2048]{0:T(1024)(128)(4,1)S(1)} %iota_compare_fusion, ...), kind=kLoop, calls=%fused_computation.6 | loop fusion | flops 8388608 | bytes 8411136 | tf_op jit(solution)/shard_map/convert_element_type | solution.py:125
  194.1 3.0 %copy.26 = f32[2048,512]{1,0:T(8,128)} copy(bf16[2048,512]{0,1:T(8,128)(2,1)S(1)} %select_convert_fusion) | data formatting | bytes 6291456 | tf_op jit(solution)/shard_map/convert_element_type | solution.py:128
  197.1 14.5 %scatter_custom_fusion.1 = f32[768,512]{1,0:T(8,128)} fusion(s32[2048]{0:T(1024)S(1)} %copy-done.9, f32[2048,512]{1,0:T(8,128)} %copy.26, f32[]{:T(128)} %constant.29.clone.1), kind=kCustom, calls=%fused_computation.35 | custom fusion | flops 1048576 | bytes 1573376 | tf_op jit(solution)/shard_map/scatter-add | solution.py:127
  211.6 1.5 convert.13
  213.1 0.7 fusion.83
  213.8 0.7 collective-permute-start.6
  214.6 4.9 %collective-permute-start.7 = (bf16[256,512]{1,0:T(8,128)(2,1)S(1)}, bf16[256,512]{1,0:T(8,128)(2,1)}, u32[]{:S(2)}, u32[]{:S(2)}) collective-permute-start(bf16[256,512]{1,0:T(8,128)(2,1)S(1)} %get-tuple-element.19), channel_id=1, source_target_pairs={{1,0},{2,1},{3,2},{4,3},{5,4},{6,5},{7,6},{8,7},{9,8},{10,9},{11,1... | collective-permute-start | bytes 786440 | tf_op jit(solution)/shard_map/ppermute | solution.py:40
  219.5 1.3 fusion.31
  220.8 2.5 %copy.27 = bf16[2048,512]{1,0:T(8,128)(2,1)} copy(bf16[2048,512]{0,1:T(8,128)(2,1)S(1)} %select_convert_fusion) | data formatting | bytes 4194304
  223.3 0.8 collective-permute-done.6
  224.1 2.1 collective-permute-done.7
  226.3 2.1 fusion.103
  228.4 0.2 multiply_reduce_fusion.2
  228.6 0.9 add_convert_fusion
  (56 shorter events, 0.3 us)
Async XLA Ops:
  0.6 2.8 %copy-start.6 = (bf16[256,512]{1,0:T(8,128)(2,1)S(1)}, bf16[256,512]{1,0:T(8,128)(2,1)}, u32[]{:S(2)}) copy-start(bf16[256,512]{1,0:T(8,128)(2,1)} %param.20) | copy-start | bytes 786436
  3.3 9.2 %copy-start.16 = (s32[2,1]{0,1:T(1,128)S(1)}, s32[2,1]{0,1:T(1,128)}, u32[]{:S(2)}) copy-start(s32[2,1]{0,1:T(1,128)} %param.25) | copy-start | bytes 28
  3.3 46.8 %copy-start.8 = (s32[2048]{0:T(1024)S(1)}, s32[2048]{0:T(1024)}, u32[]{:S(2)}) copy-start(s32[2048]{0:T(1024)} %param.22) | copy-start | bytes 24580
  3.3 46.9 %copy-start.10 = (f32[2,512]{1,0:T(2,128)S(1)}, f32[2,512]{1,0:T(2,128)}, u32[]{:S(2)}) copy-start(f32[2,512]{1,0:T(2,128)} %param.27) | copy-start | bytes 12292
  3.3 46.9 %copy-start.11 = (f32[2,512]{1,0:T(2,128)S(1)}, f32[2,512]{1,0:T(2,128)}, u32[]{:S(2)}) copy-start(f32[2,512]{1,0:T(2,128)} %param.29) | copy-start | bytes 12292
  3.4 46.9 %copy-start.12 = (f32[2,512]{1,0:T(2,128)S(1)}, f32[2,512]{1,0:T(2,128)}, u32[]{:S(2)}) copy-start(f32[2,512]{1,0:T(2,128)} %param.30) | copy-start | bytes 12292
  3.4 47.5 %copy-start.5 = (bf16[2048,512]{1,0:T(8,128)(2,1)S(1)}, bf16[2048,512]{1,0:T(8,128)(2,1)}, u32[]{:S(2)}) copy-start(bf16[2048,512]{1,0:T(8,128)(2,1)} %param.21) | copy-start | bytes 6291460
  3.8 49.6 %collective-permute-start = (bf16[256,1024]{1,0:T(8,128)(2,1)S(1)}, bf16[256,1024]{1,0:T(8,128)(2,1)}, u32[]{:S(2)}, u32[]{:S(2)}) collective-permute-start(bf16[256,1024]{1,0:T(8,128)(2,1)S(1)} %fusion.6), channel_id=1, source_target_pairs={{0,1},{1,2},{2,3},{3,4},{4,5},{5,6},{6,7},{7,8},{8,9},{9,10},{10,1... | collective-permute-start | bytes 1572872 | tf_op jit(solution)/shard_map/ppermute | solution.py:21
  7.1 46.3 %collective-permute-start.1 = (bf16[256,1024]{1,0:T(8,128)(2,1)S(1)}, bf16[256,1024]{1,0:T(8,128)(2,1)}, u32[]{:S(2)}, u32[]{:S(2)}) collective-permute-start(bf16[256,1024]{1,0:T(8,128)(2,1)S(1)} %fusion.6), channel_id=1, source_target_pairs={{1,0},{2,1},{3,2},{4,3},{5,4},{6,5},{7,6},{8,7},{9,8},{10,9},{11,1... | collective-permute-start | bytes 1572872 | tf_op jit(solution)/shard_map/ppermute | solution.py:23
  50.9 2.4 %copy-start.13 = (f32[2,512]{1,0:T(2,128)S(1)}, f32[2,512]{1,0:T(2,128)}, u32[]{:S(2)}) copy-start(f32[2,512]{1,0:T(2,128)} %param.32) | copy-start | bytes 12292
  50.9 2.4 %copy-start.14 = (f32[2,512]{1,0:T(2,128)S(1)}, f32[2,512]{1,0:T(2,128)}, u32[]{:S(2)}) copy-start(f32[2,512]{1,0:T(2,128)} %param.34) | copy-start | bytes 12292
  50.9 2.4 %copy-start.9 = (s32[2048]{0:T(1024)S(1)}, s32[2048]{0:T(1024)}, u32[]{:S(2)}) copy-start(s32[2048]{0:T(1024)} %param.23) | copy-start | bytes 24580
  64.1 9.2 %copy-start.4 = (bf16[2048,512]{1,0:T(8,128)(2,1)S(1)}, bf16[2048,512]{1,0:T(8,128)(2,1)}, u32[]{:S(2)}) copy-start(bf16[2048,512]{1,0:T(8,128)(2,1)} %gather_fusion) | copy-start | bytes 6291460
  79.9 3.4 %copy-start.3 = (f32[2048,512]{0,1:T(8,128)S(1)}, f32[2048,512]{0,1:T(8,128)}, u32[]{:S(2)}) copy-start(f32[2048,512]{0,1:T(8,128)} %get-tuple-element.37) | copy-start | bytes 12582916
  86.2 3.1 %copy-start = (bf16[2048,512]{0,1:T(8,128)(2,1)}, bf16[2048,512]{0,1:T(8,128)(2,1)S(1)}, u32[]{:S(2)}) copy-start(bf16[2048,512]{0,1:T(8,128)(2,1)S(1)} %select_convert_fusion.1) | copy-start | bytes 6291460
  103.6 7.4 %copy-start.15 = (f32[2,512]{1,0:T(2,128)S(1)}, f32[2,512]{1,0:T(2,128)}, u32[]{:S(2)}) copy-start(f32[2,512]{1,0:T(2,128)} %param.35) | copy-start | bytes 12292
  103.7 7.4 %copy-start.7 = (bf16[2,2,512,512]{3,2,1,0:T(8,128)(2,1)S(1)}, bf16[2,2,512,512]{3,2,1,0:T(8,128)(2,1)}, u32[]{:S(2)}) copy-start(bf16[2,2,512,512]{3,2,1,0:T(8,128)(2,1)} %param.31) | copy-start | bytes 6291460
  105.4 10.2 %collective-permute-start.2 = (bf16[256,512]{1,0:T(8,128)(2,1)S(1)}, bf16[256,512]{1,0:T(8,128)(2,1)S(1)}, u32[]{:S(2)}, u32[]{:S(2)}) collective-permute-start(bf16[256,512]{1,0:T(8,128)(2,1)S(1)} %get-tuple-element.20), channel_id=1, source_target_pairs={{15,0},{0,1},{1,2},{2,3},{3,4},{4,5},{5,6},{6,7},{7,8},{8,9},{9,10... | collective-permute-start | bytes 786440 | tf_op jit(solution)/shard_map/ppermute | solution.py:40
  105.9 12.0 %collective-permute-start.3 = (bf16[256,512]{1,0:T(8,128)(2,1)S(1)}, bf16[256,512]{1,0:T(8,128)(2,1)S(1)}, u32[]{:S(2)}, u32[]{:S(2)}) collective-permute-start(bf16[256,512]{1,0:T(8,128)(2,1)S(1)} %get-tuple-element.21), channel_id=1, source_target_pairs={{1,0},{2,1},{3,2},{4,3},{5,4},{6,5},{7,6},{8,7},{9,8},{10,9},{11,1... | collective-permute-start | bytes 786440 | tf_op jit(solution)/shard_map/ppermute | solution.py:40
  115.5 2.3 %copy-start.17 = (bf16[256,512]{1,0:T(8,128)(2,1)}, bf16[256,512]{1,0:T(8,128)(2,1)S(1)}, u32[]{:S(2)}) copy-start(bf16[256,512]{1,0:T(8,128)(2,1)S(1)} %collective-permute-done.2) | copy-start | bytes 786436
  117.9 0.7 copy-start.18
  122.7 38.6 %collective-permute-start.4 = (bf16[256,1024]{1,0:T(8,128)(2,1)S(1)}, bf16[256,1024]{1,0:T(8,128)(2,1)S(1)}, u32[]{:S(2)}, u32[]{:S(2)}) collective-permute-start(bf16[256,1024]{1,0:T(8,128)(2,1)S(1)} %convolution_convert_fusion.1), channel_id=1, source_target_pairs={{0,1},{1,2},{2,3},{3,4},{4,5},{5,6},{6,7},{7,8},{8,9},{9,10},{10,1... | collective-permute-start | bytes 1572872 | tf_op jit(solution)/shard_map/ppermute | solution.py:21
  124.4 36.9 %collective-permute-start.5 = (bf16[256,1024]{1,0:T(8,128)(2,1)S(1)}, bf16[256,1024]{1,0:T(8,128)(2,1)S(1)}, u32[]{:S(2)}, u32[]{:S(2)}) collective-permute-start(bf16[256,1024]{1,0:T(8,128)(2,1)S(1)} %convolution_convert_fusion.1), channel_id=1, source_target_pairs={{1,0},{2,1},{3,2},{4,3},{5,4},{6,5},{7,6},{8,7},{9,8},{10,9},{11,1... | collective-permute-start | bytes 1572872 | tf_op jit(solution)/shard_map/ppermute | solution.py:23
  170.8 9.2 %copy-start.1 = (bf16[2048,512]{0,1:T(8,128)(2,1)S(1)}, bf16[2048,512]{0,1:T(8,128)(2,1)}, u32[]{:S(2)}) copy-start(bf16[2048,512]{0,1:T(8,128)(2,1)} %copy-done) | copy-start | bytes 6291460
  187.9 2.9 %copy-start.2 = (bf16[2048,512]{0,1:T(8,128)(2,1)S(1)}, bf16[2048,512]{0,1:T(8,128)(2,1)}, u32[]{:S(2)}) copy-start(bf16[2048,512]{0,1:T(8,128)(2,1)} %copy-done) | copy-start | bytes 6291460
  213.8 10.3 %collective-permute-start.6 = (bf16[256,512]{1,0:T(8,128)(2,1)}, bf16[256,512]{1,0:T(8,128)(2,1)S(1)}, u32[]{:S(2)}, u32[]{:S(2)}) collective-permute-start(bf16[256,512]{1,0:T(8,128)(2,1)} %get-tuple-element.18), channel_id=1, source_target_pairs={{15,0},{0,1},{1,2},{2,3},{3,4},{4,5},{5,6},{6,7},{7,8},{8,9},{9,10... | collective-permute-start | bytes 786440 | tf_op jit(solution)/shard_map/ppermute | solution.py:40
  214.6 11.7 %collective-permute-start.7 = (bf16[256,512]{1,0:T(8,128)(2,1)S(1)}, bf16[256,512]{1,0:T(8,128)(2,1)}, u32[]{:S(2)}, u32[]{:S(2)}) collective-permute-start(bf16[256,512]{1,0:T(8,128)(2,1)S(1)} %get-tuple-element.19), channel_id=1, source_target_pairs={{1,0},{2,1},{3,2},{4,3},{5,4},{6,5},{7,6},{8,7},{9,8},{10,9},{11,1... | collective-permute-start | bytes 786440 | tf_op jit(solution)/shard_map/ppermute | solution.py:40
